TPU v7x, 32 devices: a whole 2x2x4 slice. The times are simulated.
32 devices in a mesh: seq: 4 (over z), tensor: 2 (over y), fsdp: 4 (over x, core).
Axes of the slice: x: 2, y: 2, z: 4, core: 2. Of those that a mesh axis runs over, the one named last changes fastest.
Arguments:
- hidden_in: bfloat16 [2048, 2048], P(('seq', 'fsdp'), 'tensor'), may hold values from -12 to 12
- out_cotangent: bfloat16 [2048, 2048], P(('seq', 'fsdp'), 'tensor'), may hold values from -6 to 6
- attn_norm_gain: float32 [2048], replicated, may hold values from 0.1 to 1.9
- attn_norm_bias: float32 [2048], replicated, may hold values from -3 to 3
- mlp_norm_gain: float32 [2048], replicated, may hold values from 0.1 to 1.9
- mlp_norm_bias: float32 [2048], replicated, may hold values from -3 to 3
- qkv_weight: bfloat16 [2048, 6144], P(('seq', 'fsdp'), 'tensor')
- qkv_bias: float32 [6144], P('tensor'), may hold values from -0.6 to 0.6
- proj_weight: bfloat16 [2048, 2048], P(('seq', 'fsdp'), 'tensor'), may hold values from -1.5 to 1.5
- proj_bias: float32 [2048], P('tensor'), may hold values from -3 to 3
- up_weight: bfloat16 [2048, 8192], P(('seq', 'fsdp'), 'tensor'), may hold values from -0.125 to 0.125
- up_bias: float32 [8192], P('tensor'), may hold values from -3 to 3
- down_weight: bfloat16 [2048, 8192], P(('seq', 'fsdp'), 'tensor'), may hold values from -0.0625 to 0.0625
- down_bias: float32 [2048], P('tensor'), may hold values from -3 to 3
Outputs:
- hidden_out: bfloat16 [2048, 2048], P(('seq', 'fsdp'), 'tensor')
- input_grad: bfloat16 [2048, 2048], P(('seq', 'fsdp'), 'tensor')
- attn_gain_grad: float32 [2048], replicated
- attn_bias_grad: float32 [2048], replicated
- mlp_gain_grad: float32 [2048], replicated
- mlp_bias_grad: float32 [2048], replicated
- qkv_weight_grad: float32 [2048, 6144], P(('seq', 'fsdp'), 'tensor')
- qkv_bias_grad: float32 [6144], P('tensor')
- proj_weight_grad: float32 [2048, 2048], P(('seq', 'fsdp'), 'tensor')
- proj_bias_grad: float32 [2048], P('tensor')
- up_weight_grad: float32 [2048, 8192], P(('seq', 'fsdp'), 'tensor')
- up_bias_grad: float32 [8192], P('tensor')
- down_weight_grad: float32 [2048, 8192], P(('seq', 'fsdp'), 'tensor')
- down_bias_grad: float32 [2048], P('tensor')
All inputs are finite; a program needn't handle non-finite values.
Results may differ from a plain program's by a relative error of at most 0.013.
Values may be sent and summed in bfloat16 or wider, within the bound.
A program may use at most 256 MiB of HBM per device.

v0:
```python
import math
import jax
import jax.numpy as jnp
from jax import lax
from jax.sharding import PartitionSpec as P

HEAD_DIM = 256
ROT = 64
norm_eps = 1e-05
rope_base = 10000.0


def gelu_value(pre_act):
    return 0.5 * pre_act * (1.0 + lax.erf(pre_act * 0.7071067811865476))


def gelu_slope(pre_act):
    return (
        0.5 * (1.0 + lax.erf(pre_act * 0.7071067811865476))
        + pre_act * jnp.exp(-0.5 * pre_act * pre_act) * 0.3989422804014327
    )


def layer_norm_parts(row_values):
    centered = row_values - jnp.mean(row_values, axis=-1, keepdims=True)
    inv_std = lax.rsqrt(jnp.mean(centered * centered, axis=-1, keepdims=True) + norm_eps)
    return (centered * inv_std, inv_std)


def rotary_tables(positions):
    half_rot = ROT // 2
    exponent = jnp.arange(half_rot, dtype=jnp.float32) * (2.0 / ROT)
    frequency = jnp.exp(-exponent * math.log(rope_base))
    angles = positions.astype(jnp.float32)[:, None] * frequency[None, :]
    return (jnp.cos(angles), jnp.sin(angles))


def rotate_heads(values, cosine_table, sine_table):
    half_rot = ROT // 2
    first_half = values[..., :half_rot]
    second_half = values[..., half_rot:ROT]
    cos_part = cosine_table[:, None, :]
    sin_part = sine_table[:, None, :]
    return jnp.concatenate(
        [
            first_half * cos_part - second_half * sin_part,
            second_half * cos_part + first_half * sin_part,
            values[..., ROT:],
        ],
        axis=-1,
    )


def contract_rows(left_side, right_side):
    return lax.dot_general(
        left_side, right_side, (((0,), (0,)), ((), ())), preferred_element_type=jnp.float32
    )


def contract_cols(left_side, right_side):
    return lax.dot_general(
        left_side, right_side, (((1,), (1,)), ((), ())), preferred_element_type=jnp.float32
    )


def per_device(
    hidden_in,
    out_cotangent,
    attn_norm_gain,
    attn_norm_bias,
    mlp_norm_gain,
    mlp_norm_bias,
    qkv_weight,
    qkv_bias,
    proj_weight,
    proj_bias,
    up_weight,
    up_bias,
    down_weight,
    down_bias,
):
    seq_count = lax.axis_size("seq")
    fsdp_count = lax.axis_size("fsdp")
    seq_rank = lax.axis_index("seq")
    fsdp_rank = lax.axis_index("fsdp")
    tensor_rank = lax.axis_index("tensor")
    tok_rows = hidden_in.shape[0]
    local_width = hidden_in.shape[1]
    score_scale = HEAD_DIM ** (-0.5)
    rows_whole, grad_whole = (
        lax.all_gather(hidden_in, "tensor", axis=1, tiled=True),
        lax.all_gather(out_cotangent, "tensor", axis=1, tiled=True),
    )
    float_rows = rows_whole.astype(jnp.float32)
    normal_rows, inv_std = layer_norm_parts(float_rows)
    attn_in = (normal_rows * attn_norm_gain + attn_norm_bias).astype(jnp.bfloat16)
    mlp_in = (normal_rows * mlp_norm_gain + mlp_norm_bias).astype(jnp.bfloat16)
    qkv_full, proj_full, up_full, down_full = (
        lax.all_gather(qkv_weight, ("seq", "fsdp"), axis=0, tiled=True),
        lax.all_gather(proj_weight, ("seq", "fsdp"), axis=0, tiled=True),
        lax.all_gather(up_weight, ("seq", "fsdp"), axis=0, tiled=True),
        lax.all_gather(down_weight, ("seq", "fsdp"), axis=0, tiled=True),
    )
    local_heads = local_width // HEAD_DIM
    head_share = local_heads // seq_count
    qkv_rows = jnp.dot(attn_in, qkv_full, preferred_element_type=jnp.float32) + qkv_bias
    qkv_rows = qkv_rows.reshape(tok_rows, local_heads, 3, HEAD_DIM)
    positions = (seq_rank * fsdp_count + fsdp_rank) * tok_rows + jnp.arange(
        tok_rows, dtype=jnp.int32
    )
    cosine_table, sine_table = rotary_tables(positions)
    packed = jnp.concatenate(
        [
            rotate_heads(qkv_rows[:, :, 0], cosine_table, sine_table),
            rotate_heads(qkv_rows[:, :, 1], cosine_table, sine_table),
            qkv_rows[:, :, 2],
        ],
        axis=-1,
    ).astype(jnp.bfloat16)
    by_head = lax.all_to_all(packed, "seq", split_axis=1, concat_axis=0, tiled=True)
    head_rows = by_head.shape[0]
    query_heads = by_head[:, :, :HEAD_DIM]
    pair_local = by_head[:, :, HEAD_DIM:]
    row_index = jnp.arange(head_rows, dtype=jnp.int32)
    query_pos = (row_index // tok_rows * fsdp_count + fsdp_rank) * tok_rows + row_index % tok_rows
    pair_all = lax.all_gather(pair_local, "fsdp", axis=0, tiled=True)
    key_rows = pair_all.shape[0]
    key_index = jnp.arange(key_rows, dtype=jnp.int32)
    within = key_index % head_rows
    key_pos = (
        within // tok_rows * fsdp_count + key_index // head_rows
    ) * tok_rows + within % tok_rows
    block_keys = math.gcd(key_rows, 1024)
    block_numbers = jnp.arange(key_rows // block_keys, dtype=jnp.int32)

    def block_scores(pair_source, block_number):
        start_row = block_number * block_keys
        pair_block = lax.dynamic_slice_in_dim(pair_source, start_row, block_keys, 0)
        pos_block = lax.dynamic_slice_in_dim(key_pos, start_row, block_keys, 0)
        scores = (
            jnp.einsum(
                "rhd,khd->rhk",
                query_heads,
                pair_block[:, :, :HEAD_DIM],
                preferred_element_type=jnp.float32,
            )
            * score_scale
        )
        allowed = pos_block[None, None, :] <= query_pos[:, None, None]
        return (pair_block, jnp.where(allowed, scores, -1e30), allowed)

    def forward_step(running, block_number):
        running_max, running_sum, accumulated = running
        pair_block, scores, allowed = block_scores(pair_all, block_number)
        new_max = jnp.maximum(running_max, jnp.max(scores, axis=-1))
        exp_terms = jnp.where(allowed, jnp.exp(scores - new_max[..., None]), 0.0)
        rescale = jnp.exp(running_max - new_max)
        running_sum = running_sum * rescale + jnp.sum(exp_terms, axis=-1)
        accumulated = accumulated * rescale[..., None] + jnp.einsum(
            "rhk,khd->rhd",
            exp_terms.astype(jnp.bfloat16),
            pair_block[:, :, HEAD_DIM:],
            preferred_element_type=jnp.float32,
        )
        return ((new_max, running_sum, accumulated), None)

    start_max = jnp.full((head_rows, head_share), -1e30, jnp.float32)
    start_sum = jnp.zeros((head_rows, head_share), jnp.float32)
    start_acc = jnp.zeros((head_rows, head_share, HEAD_DIM), jnp.float32)
    (row_max, row_sum, accumulated), ignored = lax.scan(
        forward_step, (start_max, start_sum, start_acc), block_numbers
    )
    attn_out = (accumulated / row_sum[..., None]).astype(jnp.bfloat16)
    log_total = row_max + jnp.log(row_sum)
    attn_tokens = lax.all_to_all(attn_out, "seq", split_axis=0, concat_axis=1, tiled=True).reshape(
        tok_rows, local_width
    )
    attn_branch = contract_cols(attn_tokens, proj_full)
    up_rows = jnp.dot(mlp_in, up_full, preferred_element_type=jnp.float32) + up_bias
    active = gelu_value(up_rows).astype(jnp.bfloat16)
    mlp_branch = contract_cols(active, down_full)
    branch_cols = lax.psum_scatter(
        attn_branch + mlp_branch, "tensor", scatter_dimension=1, tiled=True
    )
    hidden_out = (hidden_in.astype(jnp.float32) + branch_cols + proj_bias + down_bias).astype(
        jnp.bfloat16
    )
    qkv_back, proj_back, up_back, down_back = (
        lax.all_gather(qkv_weight, ("seq", "fsdp"), axis=0, tiled=True),
        lax.all_gather(proj_weight, ("seq", "fsdp"), axis=0, tiled=True),
        lax.all_gather(up_weight, ("seq", "fsdp"), axis=0, tiled=True),
        lax.all_gather(down_weight, ("seq", "fsdp"), axis=0, tiled=True),
    )
    pair_back = lax.all_gather(pair_local, "fsdp", axis=0, tiled=True)
    head_grad = jnp.dot(grad_whole, proj_back, preferred_element_type=jnp.float32).astype(
        jnp.bfloat16
    )
    grad_heads = lax.all_to_all(
        head_grad.reshape(tok_rows, local_heads, HEAD_DIM),
        "seq",
        split_axis=1,
        concat_axis=0,
        tiled=True,
    )
    proj_term = contract_rows(grad_whole, attn_tokens)
    pre_grad = jnp.dot(grad_whole, down_back, preferred_element_type=jnp.float32) * gelu_slope(
        up_rows
    )
    pre_rounded = pre_grad.astype(jnp.bfloat16)
    up_bias_term = jnp.sum(pre_grad, axis=0)
    up_term = contract_rows(mlp_in, pre_rounded)
    down_term = contract_rows(grad_whole, active)
    mlp_in_grad = contract_cols(pre_rounded, up_back)
    row_delta = jnp.sum(grad_heads.astype(jnp.float32) * attn_out.astype(jnp.float32), axis=-1)

    def backward_step(query_grad, block_number):
        pair_block, scores, allowed = block_scores(pair_back, block_number)
        prob_weights = jnp.where(allowed, jnp.exp(scores - log_total[..., None]), 0.0)
        prob_grad = jnp.einsum(
            "rhd,khd->rhk",
            grad_heads,
            pair_block[:, :, HEAD_DIM:],
            preferred_element_type=jnp.float32,
        )
        score_grad = (prob_weights * (prob_grad - row_delta[..., None])).astype(jnp.bfloat16)
        query_grad = query_grad + jnp.einsum(
            "rhk,khd->rhd",
            score_grad,
            pair_block[:, :, :HEAD_DIM],
            preferred_element_type=jnp.float32,
        )
        key_term = (
            jnp.einsum("rhk,rhd->khd", score_grad, query_heads, preferred_element_type=jnp.float32)
            * score_scale
        )
        value_term = jnp.einsum(
            "rhk,rhd->khd",
            prob_weights.astype(jnp.bfloat16),
            grad_heads,
            preferred_element_type=jnp.float32,
        )
        return (query_grad, jnp.concatenate([key_term, value_term], axis=-1))

    query_grad, pair_terms = lax.scan(backward_step, start_acc, block_numbers)
    pair_terms = pair_terms.reshape(key_rows, head_share, 2 * HEAD_DIM)
    pair_grad = lax.psum_scatter(pair_terms, "fsdp", scatter_dimension=0, tiled=True)
    head_cos, head_sin = rotary_tables(query_pos)
    grads_packed = jnp.concatenate(
        [
            rotate_heads(query_grad * score_scale, head_cos, -head_sin),
            rotate_heads(pair_grad[:, :, :HEAD_DIM], head_cos, -head_sin),
            pair_grad[:, :, HEAD_DIM:],
        ],
        axis=-1,
    ).astype(jnp.bfloat16)
    token_grads = lax.all_to_all(
        grads_packed, "seq", split_axis=0, concat_axis=1, tiled=True
    ).reshape(tok_rows, 3 * local_width)
    qkv_bias_term = jnp.sum(token_grads.astype(jnp.float32), axis=0)
    qkv_term = contract_rows(attn_in, token_grads)
    attn_in_grad = contract_cols(token_grads, qkv_back)
    attn_in_grad, mlp_in_grad = lax.psum((attn_in_grad, mlp_in_grad), "tensor")
    attn_gain_term = jnp.sum(attn_in_grad * normal_rows, axis=0)
    attn_bias_term = jnp.sum(attn_in_grad, axis=0)
    mlp_gain_term = jnp.sum(mlp_in_grad * normal_rows, axis=0)
    mlp_bias_term = jnp.sum(mlp_in_grad, axis=0)
    spread_grad = attn_in_grad * attn_norm_gain + mlp_in_grad * mlp_norm_gain
    mean_grad = jnp.mean(spread_grad, axis=-1, keepdims=True)
    mean_proj = jnp.mean(spread_grad * normal_rows, axis=-1, keepdims=True)
    column_start = tensor_rank * local_width
    spread_cols = lax.dynamic_slice_in_dim(spread_grad, column_start, local_width, 1)
    normal_cols = lax.dynamic_slice_in_dim(normal_rows, column_start, local_width, 1)
    grad_local = out_cotangent.astype(jnp.float32)
    input_grad = (
        grad_local + inv_std * (spread_cols - mean_grad - normal_cols * mean_proj)
    ).astype(jnp.bfloat16)
    out_bias_term = jnp.sum(grad_local, axis=0)
    qkv_weight_grad, proj_weight_grad, up_weight_grad, down_weight_grad = (
        lax.psum_scatter(qkv_term, ("seq", "fsdp"), scatter_dimension=0, tiled=True),
        lax.psum_scatter(proj_term, ("seq", "fsdp"), scatter_dimension=0, tiled=True),
        lax.psum_scatter(up_term, ("seq", "fsdp"), scatter_dimension=0, tiled=True),
        lax.psum_scatter(down_term, ("seq", "fsdp"), scatter_dimension=0, tiled=True),
    )
    (
        qkv_bias_grad,
        out_bias_grad,
        up_bias_grad,
        attn_gain_grad,
        attn_bias_grad,
        mlp_gain_grad,
        mlp_bias_grad,
    ) = lax.psum(
        (
            qkv_bias_term,
            out_bias_term,
            up_bias_term,
            attn_gain_term,
            attn_bias_term,
            mlp_gain_term,
            mlp_bias_term,
        ),
        ("seq", "fsdp"),
    )
    return (
        hidden_out,
        input_grad,
        attn_gain_grad,
        attn_bias_grad,
        mlp_gain_grad,
        mlp_bias_grad,
        qkv_weight_grad,
        qkv_bias_grad,
        proj_weight_grad,
        out_bias_grad,
        up_weight_grad,
        up_bias_grad,
        down_weight_grad,
        out_bias_grad,
    )


def solution(mesh):
    placed = (
        P(("seq", "fsdp"), "tensor"),
        P(("seq", "fsdp"), "tensor"),
        P(),
        P(),
        P(),
        P(),
        P(("seq", "fsdp"), "tensor"),
        P("tensor"),
        P(("seq", "fsdp"), "tensor"),
        P("tensor"),
        P(("seq", "fsdp"), "tensor"),
        P("tensor"),
        P(("seq", "fsdp"), "tensor"),
        P("tensor"),
    )
    return jax.shard_map(
        per_device,
        mesh=mesh,
        in_specs=placed,
        out_specs=(
            P(("seq", "fsdp"), "tensor"),
            P(("seq", "fsdp"), "tensor"),
            P(),
            P(),
            P(),
            P(),
            P(("seq", "fsdp"), "tensor"),
            P("tensor"),
            P(("seq", "fsdp"), "tensor"),
            P("tensor"),
            P(("seq", "fsdp"), "tensor"),
            P("tensor"),
            P(("seq", "fsdp"), "tensor"),
            P("tensor"),
        ),
        check_vma=False,
    )
```

profile of v0, /device:TPU:0, one launch (start us, length us, event | category | flops | bytes accessed | tf_op | source)
XLA Modules:
  0.0 1770.2 jit_solution(5235780684351520265)
XLA Ops:
  8.8 10.2 all_gather.26
  19.6 93.9 %all-gather.6.cloned.1.call-done = bf16[2048,3072]{1,0:T(8,128)(2,1)} async-done(((bf16[128,3072]{1,0:T(8,128)(2,1)}), bf16[2048,3072]{1,0:T(8,128)(2,1)}) %all-gather.6.cloned.1.call-update) | async-done | bytes 12582928 | tf_op jit(solution)/shard_map/all_gather | solution.py:99
  125.8 33.6 %all_to_all.66 = bf16[128,4,768]{2,0,1:T(8,128)(2,1)S(1)} all-to-all(bf16[128,4,768]{2,0,1:T(8,128)(2,1)S(1)} %concatenate.20), channel_id=1, replica_groups=mesh['seq'=4,'tensor'=2,'fsdp'=4] {'seq'}, dimensions={1} | all-to-all | bytes 1572864 | tf_op jit(solution)/shard_map/all_to_all | solution.py:120
  177.5 16.9 all-gather.8.cloned.1.call-done
  194.4 11.1 while.28
  206.6 28.2 %while.29 = (s32[]{:T(128)}, f32[512,1,256]{0,2,1:T(8,128)}, f32[2,1024,1,512]{3,1,0,2:T(8,128)}, s32[2]{0:T(128)S(1)}, bf16[2048,1,512]{2,0,1:T(8,128)(2,1)}, /...) while((s32[]{:T(128)}, f32[512,1,256]{0,2,1:T(8,128)}, ...), condition=%wide.region_9.10_spmd.clone, body=%wide.region_8.9_spmd.clone.sunk | while | flops 1347952640 | bytes 34100076 | solution.py:244
  240.3 10.9 all-gather.14.cloned.1.call-start
  252.0 70.9 %all-gather.12.cloned.1.call-done = bf16[2048,4096]{1,0:T(8,128)(2,1)} async-done(((bf16[128,4096]{1,0:T(8,128)(2,1)}), bf16[2048,4096]{1,0:T(8,128)(2,1)}) %all-gather.12.cloned.1.call-update) | async-done | bytes 16777232 | tf_op jit(solution)/shard_map/all_gather | solution.py:101
  331.1 36.7 %reduce-scatter.9.cloned.1.call-done = f32[512,1,512]{0,2,1:T(8,128)} async-done(((f32[2048,1,512]{0,2,1:T(8,128)}), f32[512,1,512]{0,2,1:T(8,128)}) %reduce-scatter.9.cloned.1.call-update) | async-done | bytes 1048592 | tf_op jit(solution)/shard_map/reduce_scatter | solution.py:246
  382.8 130.3 %all-gather.14.cloned.1.call-done = bf16[2048,4096]{1,0:T(8,128)(2,1)} async-done(((bf16[128,4096]{1,0:T(8,128)(2,1)}), bf16[2048,4096]{1,0:T(8,128)(2,1)}) %all-gather.14.cloned.1.call-update) | async-done | bytes 16777232 | tf_op jit(solution)/shard_map/all_gather | solution.py:102
  513.1 10.6 fusion.133
  523.7 12.7 fusion.73
  544.9 10.1 fusion.134
  557.6 12.9 all_to_all.67
  574.4 12.5 fusion.129
  594.0 22.4 %all-reduce.7.cloned.1.call-done = (f32[128,2048]{1,0:T(8,128)}, f32[128,2048]{1,0:T(8,128)}) async-done(((f32[128,2048]{1,0:T(8,128)}, f32[128,2048]{1,0:T(8,128)}), (f32[128,2048]{1,0:T(8,128)}, f32[128,2048]{1,0:T(8,128)})) %all-reduce.7.cloned.1.call-update) | async-done | bytes 2097168 | tf_op jit(solution)/shard_map/psum | solution.py:262
  625.6 13.3 convolution_bitcast_fusion.3
  640.0 10.2 fusion.128
  651.4 13.3 fusion.71
  667.5 65.7 %all-reduce.5.cloned.1.call-done = (f32[2048]{0:T(1024)}, f32[2048]{0:T(1024)}, f32[2048]{0:T(1024)}, f32[2048]{0:T(1024)}, f32[3072]{0:T(1024)}, /*index=5*/f32[1024]{0:T(1024)}, f32[4096]{0:T(1024)}) async-done(((f32[2048]{0:T(1024)}, f32[2048]{0:T(1024)}, f32[2048]{0:T(1024)}, f32[2048]{0:T(1024)}, f32[3072]{0:T(1024)}, /*index=5*/f32[1024]{0:T(1024)}, f32[4096]{0:T(1024)}), (f32[2048]{0:T(1024)}, ...) | async-done | bytes 65552 | tf_op jit(solution)/shard_map/psum | solution.py:292
  733.2 109.3 %reduce-scatter.13.cloned.1.call-done = f32[128,1024]{0,1:T(8,128)} async-done(((f32[2048,1024]{0,1:T(8,128)}), f32[128,1024]{0,1:T(8,128)}) %reduce-scatter.13.cloned.1.call-update) | async-done | bytes 524304 | tf_op jit(solution)/shard_map/reduce_scatter | solution.py:280
  844.6 332.1 %reduce-scatter.17.cloned.1.call-done = f32[128,4096]{0,1:T(8,128)} async-done(((f32[2048,4096]{0,1:T(8,128)}), f32[128,4096]{0,1:T(8,128)}) %reduce-scatter.17.cloned.1.call-update) | async-done | bytes 2097168 | tf_op jit(solution)/shard_map/reduce_scatter | solution.py:282
  1179.6 244.3 %reduce-scatter.11.cloned.1.call-done = f32[128,3072]{1,0:T(8,128)} async-done(((f32[2048,3072]{1,0:T(8,128)}), f32[128,3072]{1,0:T(8,128)}) %reduce-scatter.11.cloned.1.call-update) | async-done | bytes 1572880 | tf_op jit(solution)/shard_map/reduce_scatter | solution.py:279
  1423.9 334.5 %reduce-scatter.15.cloned.1.call-done = f32[128,4096]{1,0:T(8,128)} async-done(((f32[2048,4096]{1,0:T(8,128)}), f32[128,4096]{1,0:T(8,128)}) %reduce-scatter.15.cloned.1.call-update) | async-done | bytes 2097168 | tf_op jit(solution)/shard_map/reduce_scatter | solution.py:281
  (215 shorter events, 145.2 us)
Async XLA Ops:
  7.2 106.3 %copy-start.16 = (f32[2048]{0:T(1024)S(1)}, f32[2048]{0:T(1024)}, u32[]{:S(2)}) copy-start(f32[2048]{0:T(1024)} %param.20) | copy-start | bytes 24580
  7.2 106.3 %all-gather.6.cloned.1.call-start = ((), (), s32[]{:S(2)}) async-start(), calls=%async_computation.10 | async-start | bytes 13369344 | tf_op jit(solution)/shard_map/all_gather | solution.py:99
  7.9 162.4 %all-gather.10.cloned.1.call-start = ((), (), s32[]{:S(2)}) async-start(), calls=%async_computation.12 | async-start | bytes 4456448 | tf_op jit(solution)/shard_map/all_gather | solution.py:100
  8.7 185.7 %all-gather.8.cloned.1.call-start = ((), (), s32[]{:S(2)}) async-start(), calls=%async_computation.11 | async-start | bytes 2621440 | tf_op jit(solution)/shard_map/all_gather | solution.py:126
  160.2 162.6 %all-gather.12.cloned.1.call-start = ((), (), s32[]{:S(2)}) async-start(), calls=%async_computation.13 | async-start | bytes 17825792 | tf_op jit(solution)/shard_map/all_gather | solution.py:101
  174.0 31.7 %all-to-all-start.2 = ((bf16[128,4,256]{2,0,1:T(8,128)(2,1)}), bf16[128,4,256]{2,0,1:T(8,128)(2,1)S(1)}, u32[]{:S(2)}, u32[]{:S(2)}) async-start(bf16[128,4,256]{2,0,1:T(8,128)(2,1)} %bitcast.160), calls=%async_computation.3 | async-start | bytes 524288 | tf_op jit(solution)/shard_map/all_to_all | solution.py:198
  177.4 190.4 %reduce-scatter.9.cloned.1.call-start = ((), (), s32[]{:S(2)}) async-start(), calls=%async_computation.16 | async-start | bytes 5242880 | tf_op jit(solution)/shard_map/reduce_scatter | solution.py:246
  240.3 272.8 %all-gather.14.cloned.1.call-start = ((), (), s32[]{:S(2)}) async-start(), calls=%async_computation.14 | async-start | bytes 17825792 | tf_op jit(solution)/shard_map/all_gather | solution.py:102
  373.9 139.2 %copy-start.8 = (bf16[128,2048]{1,0:T(8,128)(2,1)S(1)}, bf16[128,2048]{1,0:T(8,128)(2,1)}, u32[]{:S(2)}) copy-start(bf16[128,2048]{1,0:T(8,128)(2,1)} %copy-done.7) | copy-start | bytes 1572868
  378.2 158.1 %all-to-all-start.3 = ((bf16[4,2,49152]{2,1,0:T(2,128)(2,1)}), bf16[4,2,49152]{2,1,0:T(2,128)(2,1)}, u32[]{:S(2)}, u32[]{:S(2)}) async-start(bf16[4,2,49152]{2,1,0:T(2,128)(2,1)} %reshape.506), calls=%async_computation.5 | async-start | bytes 1572864 | tf_op jit(solution)/shard_map/all_to_all | solution.py:256
  382.8 233.5 %all-reduce.7.cloned.1.call-start = ((), (), s32[]{:S(2)}) async-start(), calls=%async_computation.22 | async-start | bytes 4194304 | tf_op jit(solution)/shard_map/psum | solution.py:262
  555.0 109.8 %reduce-scatter.7.cloned.1.call-start = ((), (), s32[]{:S(2)}) async-start(), calls=%async_computation.15 | async-start | bytes 1572864 | tf_op jit(solution)/shard_map/reduce_scatter | solution.py:182
  591.9 141.3 %all-reduce.5.cloned.1.call-start = ((), (), s32[]{:S(2)}) async-start(), calls=%async_computation.21 | async-start | bytes 131072 | tf_op jit(solution)/shard_map/psum | solution.py:292
  620.9 221.6 %reduce-scatter.13.cloned.1.call-start = ((), (), s32[]{:S(2)}) async-start(), calls=%async_computation.18 | async-start | bytes 8912896 | tf_op jit(solution)/shard_map/reduce_scatter | solution.py:280
  625.5 551.2 %reduce-scatter.17.cloned.1.call-start = ((), (), s32[]{:S(2)}) async-start(), calls=%async_computation.20 | async-start | bytes 35651584 | tf_op jit(solution)/shard_map/reduce_scatter | solution.py:282
  638.9 785.0 %reduce-scatter.11.cloned.1.call-start = ((), (), s32[]{:S(2)}) async-start(), calls=%async_computation.17 | async-start | bytes 26738688 | tf_op jit(solution)/shard_map/reduce_scatter | solution.py:279
  650.2 1108.2 %reduce-scatter.15.cloned.1.call-start = ((), (), s32[]{:S(2)}) async-start(), calls=%async_computation.19 | async-start | bytes 35651584 | tf_op jit(solution)/shard_map/reduce_scatter | solution.py:281
  844.5 913.9 %copy-start.20 = (f32[1024]{0:T(1024)S(1)}, f32[1024]{0:T(1024)}, u32[]{:S(2)}) copy-start(f32[1024]{0:T(1024)} %get-tuple-element.611) | copy-start | bytes 12292
  844.5 914.5 %copy-start.26 = (f32[2048]{0:T(1024)S(1)}, f32[2048]{0:T(1024)}, u32[]{:S(2)}) copy-start(f32[2048]{0:T(1024)} %get-tuple-element.604) | copy-start | bytes 24580
  844.5 915.1 %copy-start.25 = (f32[2048]{0:T(1024)S(1)}, f32[2048]{0:T(1024)}, u32[]{:S(2)}) copy-start(f32[2048]{0:T(1024)} %get-tuple-element.605) | copy-start | bytes 24580
  844.5 915.7 %copy-start.24 = (f32[2048]{0:T(1024)S(1)}, f32[2048]{0:T(1024)}, u32[]{:S(2)}) copy-start(f32[2048]{0:T(1024)} %get-tuple-element.606) | copy-start | bytes 24580
  844.5 916.3 %copy-start.23 = (f32[2048]{0:T(1024)S(1)}, f32[2048]{0:T(1024)}, u32[]{:S(2)}) copy-start(f32[2048]{0:T(1024)} %get-tuple-element.607) | copy-start | bytes 24580
  844.5 916.9 %copy-start.22 = (f32[3072]{0:T(1024)S(1)}, f32[3072]{0:T(1024)}, u32[]{:S(2)}) copy-start(f32[3072]{0:T(1024)} %get-tuple-element.609) | copy-start | bytes 36868
  844.5 918.1 %copy-start.19 = (f32[4096]{0:T(1024)S(1)}, f32[4096]{0:T(1024)}, u32[]{:S(2)}) copy-start(f32[4096]{0:T(1024)} %get-tuple-element.613) | copy-start | bytes 49156
  (24 other events, 718.0 us)
Sparse Core Ops, SparseCore 0:
  10.3 103.1 all-gather.5
  115.7 54.6 all-gather.9
  172.5 21.8 all-gather.7
  196.4 126.4 all-gather.11
  325.2 42.5 reduce-scatter.8
  369.9 143.1 all-gather.13
  555.2 61.1 all-reduce.6
  619.2 20.3 reduce-scatter.6
  645.2 87.9 all-reduce.4
  737.1 105.3 reduce-scatter.12
  846.7 329.9 reduce-scatter.16
  1181.2 242.6 reduce-scatter.10
  1428.7 329.6 reduce-scatter.14
where the time goes:
time: 1780 us; the launch traced here: 1770 us
  waiting for transfers between devices  1460 us (82%)
  matrix products  131 us (7%)
  blocking collectives  64.9 us (4%)
  local copies, waits for them, and re-layouts  59.3 us (3%)
  starting transfers between devices  19.6 us (1%)
    reduce_scatter x1, waiting for transfers between devices, per_device(): lax.psum_scatter(up_term, ('seq', 'fsdp'), scatter_dimension=0, tiled=True)  335 us
    reduce_scatter x1, waiting for transfers between devices, per_device(): lax.psum_scatter(down_term, ('seq', 'fsdp'), scatter_dimension=0, tiled=T...  332 us
    reduce_scatter x1, waiting for transfers between devices, per_device(): lax.psum_scatter(qkv_term, ('seq', 'fsdp'), scatter_dimension=0, tiled=True)  244 us
    all_gather x1, waiting for transfers between devices, per_device(): lax.all_gather(down_weight, ('seq', 'fsdp'), axis=0, tiled=True)  130 us
    reduce_scatter x1, waiting for transfers between devices, per_device(): lax.psum_scatter(proj_term, ('seq', 'fsdp'), scatter_dimension=0, tiled=T...  109 us
    all_gather x1, waiting for transfers between devices, per_device(): lax.all_gather(qkv_weight, ('seq', 'fsdp'), axis=0, tiled=True)  93.9 us
    all_gather x1, waiting for transfers between devices, per_device(): lax.all_gather(up_weight, ('seq', 'fsdp'), axis=0, tiled=True)  70.9 us
    psum x1, waiting for transfers between devices, per_device(): lax.psum((qkv_bias_term, out_bias_term, up_bias_term, attn_gain_term, att...  65.7 us
  transfers between devices with their start and end apart: 15, of which 12 were waited for; matrix products, arithmetic and copies ran while one was open for 10% of the time, Pallas kernels for 0%

commit v1 on v0

--- a/solution.py
+++ b/solution.py
@@ -8,6 +8,35 @@
 ROT = 64
 norm_eps = 1e-05
 rope_base = 10000.0
+
+
+def supply_runs(packet):
+    mesh_dim = ("seq", "fsdp")
+    outcome_arr = lax.axis_size(mesh_dim)
+    big = lax.axis_index(mesh_dim)
+    z1, passed, x_new = (outcome_arr, big, packet.shape[0])
+    z_new = jnp.zeros(
+        [dev_i * z1 if k == 0 else dev_i for k, dev_i in enumerate(packet.shape)], packet.dtype
+    )
+    long_array = lax.dynamic_update_slice_in_dim(z_new, packet, passed * x_new, axis=0)
+    b_now = d_next = packet
+    for num in range(1, z1 // 2 + 1):
+        val2 = range(z1)
+        prior = map(lambda k: (k, (k + 1) % z1), val2)
+        new = list(prior)
+        b_now = lax.ppermute(b_now, axis_name=mesh_dim, perm=new)
+        long_array = lax.dynamic_update_slice_in_dim(
+            long_array, b_now, (passed - num) % z1 * x_new, axis=0
+        )
+        if 2 * num < z1:
+            z = range(z1)
+            state_now = map(lambda k: (k, (k - 1) % z1), z)
+            upper = list(state_now)
+            d_next = lax.ppermute(d_next, axis_name=mesh_dim, perm=upper)
+            long_array = lax.dynamic_update_slice_in_dim(
+                long_array, d_next, (passed + num) % z1 * x_new, axis=0
+            )
+    return long_array
 
 
 def gelu_value(pre_act):
@@ -96,7 +125,7 @@
     attn_in = (normal_rows * attn_norm_gain + attn_norm_bias).astype(jnp.bfloat16)
     mlp_in = (normal_rows * mlp_norm_gain + mlp_norm_bias).astype(jnp.bfloat16)
     qkv_full, proj_full, up_full, down_full = (
-        lax.all_gather(qkv_weight, ("seq", "fsdp"), axis=0, tiled=True),
+        supply_runs(qkv_weight),
         lax.all_gather(proj_weight, ("seq", "fsdp"), axis=0, tiled=True),
         lax.all_gather(up_weight, ("seq", "fsdp"), axis=0, tiled=True),
         lax.all_gather(down_weight, ("seq", "fsdp"), axis=0, tiled=True),

time: 1780 us -> 1930 us (1.084)
  starting transfers between devices: 19.6 us -> 76.2 us
  waiting for transfers between devices: 1460 us -> 1510 us
  blocking collectives: 64.9 us -> 91.1 us
    ppermute x0 -> x15, starting transfers between devices: none -> 71.7 us  [the longest x8 53.8 us: supply_runs(): b_now = lax.ppermute(b_now, axis_name=mesh_dim, perm=new)]
    reduce_scatter x1, waiting for transfers between devices: 109 us -> 60.7 us  [per_device(): lax.psum_scatter(proj_term, ('seq', 'fsdp'), scatter_dimension=0, tiled=T...]
    ppermute x0 -> x15, waiting for transfers between devices: none -> 48.1 us  [the longest x8 24.5 us: supply_runs(): b_now = lax.ppermute(b_now, axis_name=mesh_dim, perm=new)]
    all_gather x1, waiting for transfers between devices: 70.9 us -> 117 us  [per_device(): lax.all_gather(up_weight, ('seq', 'fsdp'), axis=0, tiled=True)]
    all_to_all x0 -> x1, blocking collectives: none -> 44.3 us  [per_device(): lax.all_to_all(grads_packed, 'seq', split_axis=0, concat_axis=1, tiled=True)]
    all_gather x1, waiting for transfers between devices: 93.9 us -> 63.2 us  [per_device(): lax.all_gather(qkv_weight, ('seq', 'fsdp'), axis=0, tiled=True)]
    psum x1, waiting for transfers between devices: 65.7 us -> 91.6 us  [per_device(): lax.psum((qkv_bias_term, out_bias_term, up_bias_term, attn_gain_term, att...]
    reduce_scatter x1, waiting for transfers between devices: 0.02 us -> 20.8 us  [per_device(): lax.psum_scatter(attn_branch + mlp_branch, 'tensor', scatter_dimension=1,...]
  transfers between devices with their start and end apart: 15 -> 29, of which waited for: 12 -> 21; matrix products, arithmetic and copies ran while one was open for 10% -> 9% of each run, Pallas kernels for 0% -> 0%
where the time goes in v1:
time: 1930 us; the launch traced here: 1920 us
  waiting for transfers between devices  1510 us (78%)
  matrix products  134 us (7%)
  blocking collectives  91.1 us (5%)
  local copies, waits for them, and re-layouts  76.3 us (4%)
  starting transfers between devices  76.2 us (4%)
    reduce_scatter x1, waiting for transfers between devices, per_device(): lax.psum_scatter(down_term, ('seq', 'fsdp'), scatter_dimension=0, tiled=T...  336 us
    reduce_scatter x1, waiting for transfers between devices, per_device(): lax.psum_scatter(up_term, ('seq', 'fsdp'), scatter_dimension=0, tiled=True)  334 us
    reduce_scatter x1, waiting for transfers between devices, per_device(): lax.psum_scatter(qkv_term, ('seq', 'fsdp'), scatter_dimension=0, tiled=True)  244 us
    all_gather x1, waiting for transfers between devices, per_device(): lax.all_gather(down_weight, ('seq', 'fsdp'), axis=0, tiled=True)  118 us
    all_gather x1, waiting for transfers between devices, per_device(): lax.all_gather(up_weight, ('seq', 'fsdp'), axis=0, tiled=True)  117 us
    psum x1, waiting for transfers between devices, per_device(): lax.psum((qkv_bias_term, out_bias_term, up_bias_term, attn_gain_term, att...  91.6 us
    all_gather x1, waiting for transfers between devices, per_device(): lax.all_gather(qkv_weight, ('seq', 'fsdp'), axis=0, tiled=True)  63.2 us
    reduce_scatter x1, waiting for transfers between devices, per_device(): lax.psum_scatter(proj_term, ('seq', 'fsdp'), scatter_dimension=0, tiled=T...  60.7 us
  transfers between devices with their start and end apart: 29, of which 21 were waited for; matrix products, arithmetic and copies ran while one was open for 9% of the time, Pallas kernels for 0%

profile of v1, /device:TPU:0, one launch (start us, length us, event | category | flops | bytes accessed | tf_op | source)
XLA Modules:
  0.0 1921.5 jit_solution(1101132286604750451)
XLA Ops:
  62.0 15.6 collective-permute-done.5
  84.1 11.9 collective-permute-start.8
  123.9 12.0 collective-permute-start.12
  142.4 13.3 collective-permute-start.14
  174.5 18.1 all_to_all.66
  208.5 13.1 all-gather.6.cloned.1.call-done
  233.7 28.1 %while.29 = (s32[]{:T(128)}, f32[512,1,256]{0,2,1:T(8,128)}, f32[2,1024,1,512]{3,1,0,2:T(8,128)}, s32[2]{0:T(128)S(1)}, bf16[2048,1,512]{2,0,1:T(8,128)(2,1)}, /...) while((s32[]{:T(128)}, f32[512,1,256]{0,2,1:T(8,128)}, ...), condition=%wide.region_9.10_spmd.clone, body=%wide.region_8.9_spmd.clone.sunk | while | flops 1347952640 | bytes 34100076 | solution.py:273
  269.8 42.0 %reduce-scatter.9.cloned.1.call-done = f32[512,1,512]{0,2,1:T(8,128)} async-done(((f32[2048,1,512]{0,2,1:T(8,128)}), f32[512,1,512]{0,2,1:T(8,128)}) %reduce-scatter.9.cloned.1.call-update) | async-done | bytes 1048592 | tf_op jit(solution)/shard_map/reduce_scatter | solution.py:275
  317.8 44.3 %all_to_all.67 = bf16[4,2,49152]{2,1,0:T(2,128)(2,1)S(1)} all-to-all(bf16[4,2,49152]{2,1,0:T(2,128)(2,1)S(1)} %reshape.506), channel_id=1, replica_groups=mesh['seq'=4,'tensor'=2,'fsdp'=4] {'seq'}, dimensions={0} | all-to-all | bytes 1572864 | tf_op jit(solution)/shard_map/all_to_all | solution.py:285
  366.2 63.2 %all-gather.14.cloned.1.call-done = bf16[2048,3072]{1,0:T(8,128)(2,1)} async-done(((bf16[128,3072]{1,0:T(8,128)(2,1)}), bf16[2048,3072]{1,0:T(8,128)(2,1)}) %all-gather.14.cloned.1.call-update) | async-done | bytes 12582928 | tf_op jit(solution)/shard_map/all_gather | solution.py:218
  439.3 116.8 %all-gather.10.cloned.1.call-done = bf16[2048,4096]{1,0:T(8,128)(2,1)} async-done(((bf16[128,4096]{1,0:T(8,128)(2,1)}), bf16[2048,4096]{1,0:T(8,128)(2,1)}) %all-gather.10.cloned.1.call-update) | async-done | bytes 16777232 | tf_op jit(solution)/shard_map/all_gather | solution.py:130
  564.4 118.4 %all-gather.12.cloned.1.call-done = bf16[2048,4096]{1,0:T(8,128)(2,1)} async-done(((bf16[128,4096]{1,0:T(8,128)(2,1)}), bf16[2048,4096]{1,0:T(8,128)(2,1)}) %all-gather.12.cloned.1.call-update) | async-done | bytes 16777232 | tf_op jit(solution)/shard_map/all_gather | solution.py:131
  693.3 12.9 fusion.73
  708.9 12.9 all_to_all.68
  730.3 12.4 fusion.129
  750.2 17.4 all-reduce.7.cloned.1.call-done
  772.2 16.0 convolution_bitcast_fusion.3
  801.3 13.3 fusion.71
  814.6 60.7 %reduce-scatter.13.cloned.1.call-done = f32[128,1024]{0,1:T(8,128)} async-done(((f32[2048,1024]{0,1:T(8,128)}), f32[128,1024]{0,1:T(8,128)}) %reduce-scatter.13.cloned.1.call-update) | async-done | bytes 524304 | tf_op jit(solution)/shard_map/reduce_scatter | solution.py:309
  877.3 20.8 %reduce-scatter.7.cloned.1.call-done = f32[128,1024]{1,0:T(8,128)} async-done(((f32[128,2048]{1,0:T(8,128)}), f32[128,1024]{1,0:T(8,128)}) %reduce-scatter.7.cloned.1.call-update) | async-done | bytes 524304 | tf_op jit(solution)/shard_map/reduce_scatter | solution.py:211
  900.0 91.6 %all-reduce.5.cloned.1.call-done = (f32[2048]{0:T(1024)}, f32[2048]{0:T(1024)}, f32[2048]{0:T(1024)}, f32[2048]{0:T(1024)}, f32[3072]{0:T(1024)}, /*index=5*/f32[1024]{0:T(1024)}, f32[4096]{0:T(1024)}) async-done(((f32[2048]{0:T(1024)}, f32[2048]{0:T(1024)}, f32[2048]{0:T(1024)}, f32[2048]{0:T(1024)}, f32[3072]{0:T(1024)}, /*index=5*/f32[1024]{0:T(1024)}, f32[4096]{0:T(1024)}), (f32[2048]{0:T(1024)}, ...) | async-done | bytes 65552 | tf_op jit(solution)/shard_map/psum | solution.py:321
  991.7 336.4 %reduce-scatter.17.cloned.1.call-done = f32[128,4096]{0,1:T(8,128)} async-done(((f32[2048,4096]{0,1:T(8,128)}), f32[128,4096]{0,1:T(8,128)}) %reduce-scatter.17.cloned.1.call-update) | async-done | bytes 2097168 | tf_op jit(solution)/shard_map/reduce_scatter | solution.py:311
  1330.9 244.3 %reduce-scatter.11.cloned.1.call-done = f32[128,3072]{1,0:T(8,128)} async-done(((f32[2048,3072]{1,0:T(8,128)}), f32[128,3072]{1,0:T(8,128)}) %reduce-scatter.11.cloned.1.call-update) | async-done | bytes 1572880 | tf_op jit(solution)/shard_map/reduce_scatter | solution.py:308
  1575.3 334.5 %reduce-scatter.15.cloned.1.call-done = f32[128,4096]{1,0:T(8,128)} async-done(((f32[2048,4096]{1,0:T(8,128)}), f32[128,4096]{1,0:T(8,128)}) %reduce-scatter.15.cloned.1.call-update) | async-done | bytes 2097168 | tf_op jit(solution)/shard_map/reduce_scatter | solution.py:310
  (267 shorter events, 272.6 us)
Async XLA Ops:
  7.2 193.5 %all-gather.8.cloned.1.call-start = ((), (), s32[]{:S(2)}) async-start(), calls=%async_computation.11 | async-start | bytes 4456448 | tf_op jit(solution)/shard_map/all_gather | solution.py:129
  7.8 29.2 %collective-permute-start.1 = (bf16[128,3072]{1,0:T(8,128)(2,1)}, bf16[128,3072]{1,0:T(8,128)(2,1)S(1)}, u32[]{:S(2)}, u32[]{:S(2)}) collective-permute-start(bf16[128,3072]{1,0:T(8,128)(2,1)} %param.24), channel_id=1, source_target_pairs={{0,27},{1,0},{2,1},{3,2},{8,3},{9,8},{10,9},{11,10},{16,11},{17,16... | collective-permute-start | bytes 2359304 | tf_op jit(solution)/shard_map/ppermute | solution.py:35
  28.1 193.5 %all-gather.6.cloned.1.call-start = ((), (), s32[]{:S(2)}) async-start(), calls=%async_computation.10 | async-start | bytes 2621440 | tf_op jit(solution)/shard_map/all_gather | solution.py:155
  37.0 22.7 %collective-permute-start.4 = (bf16[128,3072]{1,0:T(8,128)(2,1)S(1)}, bf16[128,3072]{1,0:T(8,128)(2,1)}, u32[]{:S(2)}, u32[]{:S(2)}) collective-permute-start(bf16[128,3072]{1,0:T(8,128)(2,1)S(1)} %collective-permute-done.2), channel_id=1, source_target_pairs={{0,1},{1,2},{2,3},{3,8},{8,9},{9,10},{10,11},{11,16},{16,17},{17,1... | collective-permute-start | bytes 2359304 | tf_op jit(solution)/shard_map/ppermute | solution.py:27
  54.6 23.0 %collective-permute-start.5 = (bf16[128,3072]{1,0:T(8,128)(2,1)}, bf16[128,3072]{1,0:T(8,128)(2,1)}, u32[]{:S(2)}, u32[]{:S(2)}) collective-permute-start(bf16[128,3072]{1,0:T(8,128)(2,1)} %collective-permute-done.3), channel_id=1, source_target_pairs={{0,27},{1,0},{2,1},{3,2},{8,3},{9,8},{10,9},{11,10},{16,11},{17,16... | collective-permute-start | bytes 2359304 | tf_op jit(solution)/shard_map/ppermute | solution.py:35
  59.7 24.3 %collective-permute-start.6 = (bf16[128,3072]{1,0:T(8,128)(2,1)}, bf16[128,3072]{1,0:T(8,128)(2,1)}, u32[]{:S(2)}, u32[]{:S(2)}) collective-permute-start(bf16[128,3072]{1,0:T(8,128)(2,1)} %collective-permute-done.4), channel_id=1, source_target_pairs={{0,1},{1,2},{2,3},{3,8},{8,9},{9,10},{10,11},{11,16},{16,17},{17,1... | collective-permute-start | bytes 2359304 | tf_op jit(solution)/shard_map/ppermute | solution.py:27
  77.6 21.5 %collective-permute-start.7 = (bf16[128,3072]{1,0:T(8,128)(2,1)}, bf16[128,3072]{1,0:T(8,128)(2,1)S(1)}, u32[]{:S(2)}, u32[]{:S(2)}) collective-permute-start(bf16[128,3072]{1,0:T(8,128)(2,1)} %collective-permute-done.5), channel_id=1, source_target_pairs={{0,27},{1,0},{2,1},{3,2},{8,3},{9,8},{10,9},{11,10},{16,11},{17,16... | collective-permute-start | bytes 2359304 | tf_op jit(solution)/shard_map/ppermute | solution.py:35
  84.1 24.9 %collective-permute-start.8 = (bf16[128,3072]{1,0:T(8,128)(2,1)}, bf16[128,3072]{1,0:T(8,128)(2,1)S(1)}, u32[]{:S(2)}, u32[]{:S(2)}) collective-permute-start(bf16[128,3072]{1,0:T(8,128)(2,1)} %collective-permute-done.6), channel_id=1, source_target_pairs={{0,1},{1,2},{2,3},{3,8},{8,9},{9,10},{10,11},{11,16},{16,17},{17,1... | collective-permute-start | bytes 2359304 | tf_op jit(solution)/shard_map/ppermute | solution.py:27
  99.1 21.2 %collective-permute-start.9 = (bf16[128,3072]{1,0:T(8,128)(2,1)S(1)}, bf16[128,3072]{1,0:T(8,128)(2,1)S(1)}, u32[]{:S(2)}, u32[]{:S(2)}) collective-permute-start(bf16[128,3072]{1,0:T(8,128)(2,1)S(1)} %collective-permute-done.7), channel_id=1, source_target_pairs={{0,27},{1,0},{2,1},{3,2},{8,3},{9,8},{10,9},{11,10},{16,11},{17,16... | collective-permute-start | bytes 2359304 | tf_op jit(solution)/shard_map/ppermute | solution.py:35
  123.9 18.6 collective-permute-start.12
  137.8 19.9 %collective-permute-start.13 = (bf16[128,3072]{1,0:T(8,128)(2,1)S(1)}, bf16[128,3072]{1,0:T(8,128)(2,1)S(1)}, u32[]{:S(2)}, u32[]{:S(2)}) collective-permute-start(bf16[128,3072]{1,0:T(8,128)(2,1)S(1)} %collective-permute-done.11), channel_id=1, source_target_pairs={{0,27},{1,0},{2,1},{3,2},{8,3},{9,8},{10,9},{11,10},{16,11},{17,16... | collective-permute-start | bytes 2359304 | tf_op jit(solution)/shard_map/ppermute | solution.py:35
  142.4 18.9 collective-permute-start.14
  204.5 28.4 %all-to-all-start.2 = ((bf16[128,4,256]{2,0,1:T(8,128)(2,1)}), bf16[128,4,256]{2,0,1:T(8,128)(2,1)S(1)}, u32[]{:S(2)}, u32[]{:S(2)}) async-start(bf16[128,4,256]{2,0,1:T(8,128)(2,1)} %bitcast.160), calls=%async_computation.3 | async-start | bytes 524288 | tf_op jit(solution)/shard_map/all_to_all | solution.py:227
  207.9 104.0 %reduce-scatter.9.cloned.1.call-start = ((), (), s32[]{:S(2)}) async-start(), calls=%async_computation.15 | async-start | bytes 5242880 | tf_op jit(solution)/shard_map/reduce_scatter | solution.py:275
  267.3 162.1 %all-gather.14.cloned.1.call-start = ((), (), s32[]{:S(2)}) async-start(), calls=%async_computation.16 | async-start | bytes 13369344 | tf_op jit(solution)/shard_map/all_gather | solution.py:218
  267.9 288.2 %all-gather.10.cloned.1.call-start = ((), (), s32[]{:S(2)}) async-start(), calls=%async_computation.12 | async-start | bytes 17825792 | tf_op jit(solution)/shard_map/all_gather | solution.py:130
  268.5 414.3 %all-gather.12.cloned.1.call-start = ((), (), s32[]{:S(2)}) async-start(), calls=%async_computation.13 | async-start | bytes 17825792 | tf_op jit(solution)/shard_map/all_gather | solution.py:131
  269.1 498.6 %all-reduce.7.cloned.1.call-start = ((), (), s32[]{:S(2)}) async-start(), calls=%async_computation.22 | async-start | bytes 4194304 | tf_op jit(solution)/shard_map/psum | solution.py:291
  706.3 169.0 %reduce-scatter.13.cloned.1.call-start = ((), (), s32[]{:S(2)}) async-start(), calls=%async_computation.18 | async-start | bytes 8912896 | tf_op jit(solution)/shard_map/reduce_scatter | solution.py:309
  730.3 167.9 %reduce-scatter.7.cloned.1.call-start = ((), (), s32[]{:S(2)}) async-start(), calls=%async_computation.14 | async-start | bytes 1572864 | tf_op jit(solution)/shard_map/reduce_scatter | solution.py:211
  748.2 243.4 %all-reduce.5.cloned.1.call-start = ((), (), s32[]{:S(2)}) async-start(), calls=%async_computation.21 | async-start | bytes 131072 | tf_op jit(solution)/shard_map/psum | solution.py:321
  772.2 555.9 %reduce-scatter.17.cloned.1.call-start = ((), (), s32[]{:S(2)}) async-start(), calls=%async_computation.20 | async-start | bytes 35651584 | tf_op jit(solution)/shard_map/reduce_scatter | solution.py:311
  788.3 787.0 %reduce-scatter.11.cloned.1.call-start = ((), (), s32[]{:S(2)}) async-start(), calls=%async_computation.17 | async-start | bytes 26738688 | tf_op jit(solution)/shard_map/reduce_scatter | solution.py:308
  800.1 1109.7 %reduce-scatter.15.cloned.1.call-start = ((), (), s32[]{:S(2)}) async-start(), calls=%async_computation.19 | async-start | bytes 35651584 | tf_op jit(solution)/shard_map/reduce_scatter | solution.py:310
  (41 other events, 7860.5 us)
Sparse Core Ops, SparseCore 0:
  28.2 71.4 all-gather.7
  193.6 27.8 all-gather.5
  267.4 44.4 reduce-scatter.8
  314.0 115.3 all-gather.13
  431.4 124.6 all-gather.9
  558.1 124.5 all-gather.11
  706.4 61.1 all-reduce.6
  771.7 103.5 reduce-scatter.12
  878.1 20.0 reduce-scatter.6
  903.7 87.9 all-reduce.4
  995.9 332.0 reduce-scatter.16
  1332.6 242.6 reduce-scatter.10
  1580.1 329.6 reduce-scatter.14
